TPU v7x, 32 devices: a whole 2x2x4 slice. The times are simulated.
32 devices in a mesh: dom: 32 (over z, y, x, core).
Axes of the slice: x: 2, y: 2, z: 4, core: 2. Of those that a mesh axis runs over, the one named last changes fastest.
Arguments:
- features: bfloat16 [16384, 512], P('dom'), may hold values from -6 to 6
- weights: bfloat16 [3, 512, 512], replicated, may hold values from -0.078125 to 0.078125
- halo_send: int32 [32, 32, 4], P('dom'), may hold values from 0 to 511
- nbr_index: int32 [16384, 2, 8], P('dom'), may hold values from 0 to 639
- tile_count: int32 [32], P('dom'), may hold values from 1 to 16, as said below
- edge_ends: int32 [512, 2, 256], P('dom'), may hold values from 0 to 511
- neg_ids: int32 [256], P('dom'), may hold values from 0 to 511
Outputs:
- weight_grad: float32 [3, 512, 512], replicated
- mean_loss: float32 [], replicated
- pre_grad: bfloat16 [16384, 512], P('dom')
Inputs may be any that keep to these rules, and one draw needn't show every extreme that they name: `nbr_index`: an entry below 512 names a row of the node's own partition; an entry 512 + q * 4 + k names slot k of the halo from partition q. `tile_count`: partition 32 - 1 holds 16 tiles; every other partition holds at most 8. `edge_ends`: tile slots at or past a partition's tile_count hold no edges. `neg_ids`: entry j names a row of partition j // 8.
All inputs are finite; a program needn't handle non-finite values.
Results may differ from a plain program's by a relative error of at most 0.0012.
The roundings to bfloat16 on the way count: a program that leaves them out, or rounds other values in their place, can miss the bound.
Values may be sent and summed in bfloat16 or wider, within the bound.
A program may use at most 64 MiB of HBM per device.

v0:
```python
import jax
import jax.numpy as jnp
from jax import lax
from jax.sharding import PartitionSpec as P


def swapped(x, axis, bit):
    return lax.ppermute(x, axis, [(i, i ^ 1 << bit) for i in range(lax.axis_size(axis))])


def neighbour_mean(lookup, neighbours):
    running_sum = jnp.zeros((neighbours.shape[0], lookup.shape[1]), jnp.float32)
    for column in range(neighbours.shape[1]):
        running_sum = running_sum + lookup[neighbours[:, column]].astype(jnp.float32)
    return (running_sum / neighbours.shape[1]).astype(jnp.bfloat16)


def score_tile(source, target, negatives):
    source_wide = source.astype(jnp.float32)
    target_wide = target.astype(jnp.float32)
    positive = jnp.sum(source_wide * target_wide, axis=1)
    negative = lax.dot_general(
        source, negatives, (((1,), (1,)), ((), ())), preferred_element_type=jnp.float32
    )
    count_neg = negatives.shape[0]
    tile_loss = (
        jnp.sum(jnp.logaddexp(0.0, -positive)) + jnp.sum(jnp.logaddexp(0.0, negative)) / count_neg
    )
    grad_positive = -jax.nn.sigmoid(-positive)
    grad_negative = (jax.nn.sigmoid(negative) / count_neg).astype(jnp.bfloat16)
    source_grad = grad_positive[:, None] * target_wide + jnp.dot(
        grad_negative, negatives, preferred_element_type=jnp.float32
    )
    target_grad = grad_positive[:, None] * source_wide
    negative_grad = lax.dot_general(
        grad_negative, source, (((0,), (0,)), ((), ())), preferred_element_type=jnp.float32
    )
    return (tile_loss, source_grad, target_grad, negative_grad)


def on_device(features, weights, halo_send, nbr_index, tile_count, edge_ends, neg_ids):
    feature_width = features.shape[1]
    relation_count = nbr_index.shape[1]
    outgoing = features[halo_send[0]]
    incoming = lax.all_to_all(outgoing, "dom", split_axis=0, concat_axis=0, tiled=True)
    preact = jnp.dot(features, weights[0], preferred_element_type=jnp.float32)
    lookup = jnp.concatenate([features, incoming.reshape(-1, feature_width)], 0)
    means = []
    for relation in range(relation_count):
        mean_rows = neighbour_mean(lookup, nbr_index[:, relation, :])
        means.append(mean_rows)
        preact = preact + jnp.dot(
            mean_rows, weights[relation + 1], preferred_element_type=jnp.float32
        )
    embedding = preact.astype(jnp.bfloat16)
    negatives = lax.all_gather(embedding[neg_ids], "dom", axis=0, tiled=True)
    my_tiles = tile_count[0]

    def score_local(tile_index, running):
        loss_sum, node_grad, neg_grad = running
        pair_ends = lax.dynamic_index_in_dim(edge_ends, tile_index, 0, keepdims=False)
        tile_loss, source_grad, target_grad, negative_grad = score_tile(
            embedding[pair_ends[0]], embedding[pair_ends[1]], negatives
        )
        node_grad = node_grad.at[pair_ends[0]].add(source_grad).at[pair_ends[1]].add(target_grad)
        return (loss_sum + tile_loss, node_grad, neg_grad + negative_grad)

    initial = (
        jnp.zeros((), jnp.float32),
        jnp.zeros(features.shape, jnp.float32),
        jnp.zeros(negatives.shape, jnp.float32),
    )
    far_bit = lax.axis_size("dom").bit_length() - 2
    partner_embed, partner_ends, partner_count = swapped(
        (embedding, edge_ends, tile_count), "dom", far_bit
    )
    partner_tiles = partner_count[0]
    moved_out = jnp.maximum(my_tiles - partner_tiles, 0) // 2
    moved_in = jnp.maximum(partner_tiles - my_tiles, 0) // 2
    loss_sum, node_grad, neg_grad = lax.fori_loop(0, my_tiles - moved_out, score_local, initial)
    first_moved = partner_tiles - moved_in

    def score_table(tile_index, running):
        moved_loss, moved_neg, table = running
        pair_ends = lax.dynamic_index_in_dim(
            partner_ends, first_moved + tile_index, 0, keepdims=False
        )
        tile_loss, source_grad, target_grad, negative_grad = score_tile(
            partner_embed[pair_ends[0]], partner_embed[pair_ends[1]], negatives
        )
        table = table.at[pair_ends[0]].add(source_grad).at[pair_ends[1]].add(target_grad)
        return (moved_loss + tile_loss, moved_neg + negative_grad, table)

    empty_table = jnp.zeros(features.shape, jnp.float32)
    loss_sum, neg_grad, table = lax.fori_loop(
        0, moved_in, score_table, (loss_sum, neg_grad, empty_table)
    )
    node_grad = node_grad + swapped(table, "dom", far_bit)
    own_neg_grad = lax.psum_scatter(neg_grad, "dom", scatter_dimension=0, tiled=True)
    node_grad = node_grad.at[neg_ids].add(own_neg_grad)
    pre_grad = node_grad.astype(jnp.bfloat16)
    terms = [
        lax.dot_general(
            features, pre_grad, (((0,), (0,)), ((), ())), preferred_element_type=jnp.float32
        )
    ]
    for relation in range(relation_count):
        terms.append(
            lax.dot_general(
                means[relation],
                pre_grad,
                (((0,), (0,)), ((), ())),
                preferred_element_type=jnp.float32,
            )
        )
    weight_partial = jnp.stack(terms)
    edge_count = my_tiles.astype(jnp.float32) * edge_ends.shape[2]
    weight_sum, total_loss, edge_total = lax.psum((weight_partial, loss_sum, edge_count), "dom")
    return (weight_sum / edge_total, total_loss / edge_total, pre_grad)


def solution(mesh):
    placed = (
        P("dom", None),
        P(),
        P("dom", None, None),
        P("dom", None, None),
        P("dom"),
        P("dom", None, None),
        P("dom"),
    )
    return jax.shard_map(
        on_device, mesh=mesh, in_specs=placed, out_specs=(P(), P(), P("dom", None)), check_vma=False
    )
```

profile of v0, /device:TPU:0, one launch (start us, length us, event | category | flops | bytes accessed | tf_op | source)
XLA Modules:
  0.0 578.5 jit_solution(15513979333018335119)
XLA Ops:
  7.2 4.1 collective-permute-start
  12.9 2.0 gather_fusion.4
  15.6 6.1 %all-to-all-start = ((bf16[32,4,512]{2,1,0:T(4,128)(2,1)}), bf16[32,4,512]{2,1,0:T(4,128)(2,1)S(1)}, u32[]{:S(2)}, u32[]{:S(2)}) async-start(bf16[32,4,512]{2,1,0:T(4,128)(2,1)} %reshape.203), calls=%async_computation | async-start | bytes 262144 | tf_op jit(solution)/shard_map/all_to_all | solution.py:45
  27.7 2.3 all-to-all-done
  30.0 2.0 gather_fusion.20
  32.0 2.0 gather_fusion.19
  35.9 2.6 gather_fusion.17
  38.6 2.6 gather_fusion.16
  41.2 2.6 gather_fusion.15
  43.8 2.6 gather_fusion.14
  46.4 2.6 gather_fusion.13
  49.0 2.6 gather_fusion.12
  51.7 2.6 gather_fusion.11
  54.3 2.6 gather_fusion.10
  56.9 2.6 gather_fusion.9
  59.5 2.6 gather_fusion.8
  62.2 2.6 gather_fusion.7
  64.8 2.6 gather_fusion.6
  67.4 2.6 gather_fusion.5
  70.1 2.9 multiply_convert_fusion.7
  79.4 47.8 %all-gather = bf16[256,512]{1,0:T(8,128)(2,1)S(1)} all-gather(bf16[8,512]{1,0:T(8,128)(2,1)S(1)} %gather_fusion.21), channel_id=2, replica_groups=mesh['dom'=32] {'dom'}, dimensions={0}, use_global_device_ids=true | all-gather | bytes 270336 | tf_op jit(solution)/shard_map/all_gather | solution.py:56
  128.2 113.1 %while.28 = (s32[]{:T(128)}, f32[]{:T(128)}, f32[512,512]{1,0:T(8,128)S(1)}, f32[256,512]{1,0:T(8,128)}, s32[]{:T(128)}, /*index=5*/s32[16,2,256]{2,1,0:T(2,128)...) while((s32[]{:T(128)}, f32[]{:T(128)}, ...), condition=%wide.region_6.7_spmd, body=%wide.region_0.6_spmd.sunk | while | flops 204085504 | bytes 8149223 | solution.py:80
  129.0 2.3 gather_fusion.1
  131.3 2.3 gather_fusion
  137.1 2.1 convolution_add_fusion.11
  139.2 2.5 scatter_fusion
  141.7 2.6 scatter_custom_fusion.15
  145.1 2.3 gather_fusion.1
  147.4 2.3 gather_fusion
  153.3 2.1 convolution_add_fusion.11
  155.4 2.5 scatter_fusion
  157.9 2.6 scatter_custom_fusion.15
  161.3 2.3 gather_fusion.1
  163.6 2.3 gather_fusion
  169.4 2.1 convolution_add_fusion.11
  171.5 2.5 scatter_fusion
  174.0 2.6 scatter_custom_fusion.15
  177.4 2.3 gather_fusion.1
  179.8 2.3 gather_fusion
  185.6 2.1 convolution_add_fusion.11
  187.7 2.5 scatter_fusion
  190.2 2.6 scatter_custom_fusion.15
  193.6 2.3 gather_fusion.1
  195.9 2.3 gather_fusion
  201.7 2.1 convolution_add_fusion.11
  203.8 2.5 scatter_fusion
  206.3 2.6 scatter_custom_fusion.15
  209.7 2.3 gather_fusion.1
  212.1 2.3 gather_fusion
  217.9 2.1 convolution_add_fusion.11
  220.0 2.5 scatter_fusion
  222.5 2.6 scatter_custom_fusion.15
  225.9 2.3 gather_fusion.1
  228.2 2.3 gather_fusion
  234.0 2.1 convolution_add_fusion.11
  236.1 2.5 scatter_fusion
  238.6 2.6 scatter_custom_fusion.15
  241.8 15.7 %collective-permute-done.3 = f32[512,512]{1,0:T(8,128)} collective-permute-done((f32[512,512]{1,0:T(8,128)S(1)}, f32[512,512]{1,0:T(8,128)}, u32[]{:S(2)}, u32[]{:S(2)}) %collective-permute-start.3) | collective-permute-done | bytes 1048608 | tf_op jit(solution)/shard_map/ppermute | solution.py:8
  259.0 165.7 %reduce-scatter.2.cloned.1.call-done = f32[8,512]{1,0:T(8,128)} async-done(((f32[256,512]{1,0:T(8,128)}), f32[8,512]{1,0:T(8,128)}) %reduce-scatter.2.cloned.1.call-update) | async-done | bytes 16400 | tf_op jit(solution)/shard_map/reduce_scatter | solution.py:99
  427.5 2.0 pad_maximum_fusion
  429.5 38.1 %all-reduce = (f32[]{:T(128)}, f32[]{:T(128)}) all-reduce(f32[]{:T(128)S(6)} %mul.36, f32[]{:T(128)} %get-tuple-element.103), channel_id=1, replica_groups=mesh['dom'=32] {'dom'}, use_global_device_ids=true, to_apply=%region_17.18 | all-reduce | flops 2 | bytes 16 | tf_op jit(solution)/shard_map/psum | solution.py:118
  468.9 96.2 %all-reduce.3.cloned.1.call-done = f32[3,512,512]{1,2,0:T(8,128)} async-done(((f32[3,512,512]{1,2,0:T(8,128)}), f32[3,512,512]{1,2,0:T(8,128)}) %all-reduce.3.cloned.1.call-update) | async-done | bytes 3145744 | tf_op jit(solution)/shard_map/psum | solution.py:118
  565.2 2.9 broadcast_divide_fusion
  568.1 2.4 copy.17
  (121 shorter events, 40.1 us)
Async XLA Ops:
  7.2 17.3 %copy-start = (bf16[512,512]{1,0:T(8,128)(2,1)S(1)}, bf16[512,512]{1,0:T(8,128)(2,1)}, u32[]{:S(2)}) copy-start(bf16[512,512]{1,0:T(8,128)(2,1)} %param.11) | copy-start | bytes 1572868
  7.2 18.7 %collective-permute-start = (s32[1]{0:T(128)}, s32[1]{0:T(128)}, u32[]{:S(2)}, u32[]{:S(2)}) collective-permute-start(s32[1]{0:T(128)} %param.15), channel_id=1, source_target_pairs={{0,16},{1,17},{2,18},{3,19},{4,20},{5,21},{6,22},{7,23},{8,24},{9,... | collective-permute-start | bytes 20 | tf_op jit(solution)/shard_map/ppermute | solution.py:8
  11.3 229.9 %collective-permute-start.1 = (s32[16,2,256]{2,1,0:T(2,128)}, s32[16,2,256]{2,1,0:T(2,128)S(1)}, u32[]{:S(2)}, u32[]{:S(2)}) collective-permute-start(s32[16,2,256]{2,1,0:T(2,128)} %param.16), channel_id=1, source_target_pairs={{0,16},{1,17},{2,18},{3,19},{4,20},{5,21},{6,22},{7,23},{8,24},{9,... | collective-permute-start | bytes 98312 | tf_op jit(solution)/shard_map/ppermute | solution.py:8
  15.6 14.3 %all-to-all-start = ((bf16[32,4,512]{2,1,0:T(4,128)(2,1)}), bf16[32,4,512]{2,1,0:T(4,128)(2,1)S(1)}, u32[]{:S(2)}, u32[]{:S(2)}) async-start(bf16[32,4,512]{2,1,0:T(4,128)(2,1)} %reshape.203), calls=%async_computation | async-start | bytes 262144 | tf_op jit(solution)/shard_map/all_to_all | solution.py:45
  21.7 403.0 %reduce-scatter.2.cloned.1.call-start = ((), (), s32[]{:S(2)}) async-start(), calls=%async_computation.2 | async-start | bytes 540672 | tf_op jit(solution)/shard_map/reduce_scatter | solution.py:99
  70.1 3.7 copy-start.12
  70.1 4.2 copy-start.7
  70.1 4.2 copy-start.8
  70.1 4.2 copy-start.9
  70.1 4.2 copy-start.10
  70.1 4.2 copy-start.11
  73.0 0.8 copy-start.5
  74.9 0.8 copy-start.3
  76.9 164.3 %collective-permute-start.2 = (bf16[512,512]{1,0:T(8,128)(2,1)}, bf16[512,512]{1,0:T(8,128)(2,1)S(1)}, u32[]{:S(2)}, u32[]{:S(2)}) collective-permute-start(bf16[512,512]{1,0:T(8,128)(2,1)} %fusion.8), channel_id=1, source_target_pairs={{0,16},{1,17},{2,18},{3,19},{4,20},{5,21},{6,22},{7,23},{8,24},{9,... | collective-permute-start | bytes 1572872 | tf_op jit(solution)/shard_map/ppermute | solution.py:8
  241.6 184.4 %copy-start.4 = (bf16[512,512]{1,0:T(8,128)(2,1)S(1)}, bf16[512,512]{1,0:T(8,128)(2,1)}, u32[]{:S(2)}) copy-start(bf16[512,512]{1,0:T(8,128)(2,1)} %copy-done.3) | copy-start | bytes 1572868
  241.6 15.9 %collective-permute-start.3 = (f32[512,512]{1,0:T(8,128)S(1)}, f32[512,512]{1,0:T(8,128)}, u32[]{:S(2)}, u32[]{:S(2)}) collective-permute-start(f32[512,512]{1,0:T(8,128)S(1)} %get-tuple-element.101), channel_id=1, source_target_pairs={{0,16},{1,17},{2,18},{3,19},{4,20},{5,21},{6,22},{7,23},{8,24},{9,... | collective-permute-start | bytes 3145736 | tf_op jit(solution)/shard_map/ppermute | solution.py:8
  241.7 323.4 %all-reduce.3.cloned.1.call-start = ((), (), s32[]{:S(2)}) async-start(), calls=%async_computation.3 | async-start | bytes 6291456 | tf_op jit(solution)/shard_map/psum | solution.py:118
  257.5 169.0 %copy-start.6 = (bf16[512,512]{1,0:T(8,128)(2,1)S(1)}, bf16[512,512]{1,0:T(8,128)(2,1)}, u32[]{:S(2)}) copy-start(bf16[512,512]{1,0:T(8,128)(2,1)} %copy-done.5) | copy-start | bytes 1572868
  259.0 168.0 %copy-start.1 = (bf16[512,512]{1,0:T(8,128)(2,1)S(1)}, bf16[512,512]{1,0:T(8,128)(2,1)}, u32[]{:S(2)}) copy-start(bf16[512,512]{1,0:T(8,128)(2,1)} %param.11) | copy-start | bytes 1572868
  426.0 1.0 copy-start.2
Sparse Core Ops, SparseCore 0:
  241.9 182.7 reduce-scatter.1
  430.7 134.3 all-reduce.2
where the time goes:
time: 580 us; the launch traced here: 578 us
  waiting for transfers between devices  280 us (48%)
  blocking collectives  85.9 us (15%)
  local copies, waits for them, and re-layouts  84.1 us (14%)
  other arithmetic  59.4 us (10%)
  matrix products  28.4 us (5%)
  between operations  19.4 us (3%)
  starting transfers between devices  11.3 us (2%)
  loops' own time  10.2 us (2%)
    reduce_scatter x1, waiting for transfers between devices, on_device(): lax.psum_scatter(neg_grad, 'dom', scatter_dimension=0, tiled=True)  166 us
    psum x1, waiting for transfers between devices, on_device(): lax.psum((weight_partial, loss_sum, edge_count), 'dom')  96.2 us
    all_gather x1, blocking collectives, on_device(): negatives = lax.all_gather(embedding[neg_ids], 'dom', axis=0, tiled=True)  47.8 us
    gather x16, local copies, waits for them, and re-layouts, neighbour_mean(): lookup[neighbours[:, column]].astype(jnp.float32)  40 us
    psum x1, blocking collectives, on_device(): lax.psum((weight_partial, loss_sum, edge_count), 'dom')  38.1 us
    scatter-add x14, other arithmetic, score_local(): node_grad.at[pair_ends[0]].add(source_grad).at[pair_ends[1]]  35.5 us
    gather x7, local copies, waits for them, and re-layouts, score_local(): embedding[pair_ends[0]]  16.2 us
    gather x7, local copies, waits for them, and re-layouts, score_local(): embedding[pair_ends[1]]  16.2 us
  transfers between devices with their start and end apart: 7, of which 4 were waited for; matrix products, arithmetic and copies ran while one was open for 28% of the time, Pallas kernels for 0%

commit v1 on v0

v1 whole, which is shorter than its diff:
```python
import functools

import jax
import jax.numpy as jnp
from jax import lax
from jax.experimental import pallas as pl
from jax.experimental.pallas import tpu as pltpu
from jax.sharding import PartitionSpec as P

F32 = jnp.float32
BF16 = jnp.bfloat16
VMEM_LIMIT = 48 * 1024 * 1024


def whole(count):
    return [pl.BlockSpec(memory_space=pltpu.VMEM)] * count


def nn(a, b):
    return jnp.dot(a, b, preferred_element_type=F32)


def nt(a, b):
    return lax.dot_general(a, b, (((1,), (1,)), ((), ())), preferred_element_type=F32)


def tn(a, b):
    return lax.dot_general(a, b, (((0,), (0,)), ((), ())), preferred_element_type=F32)


def halves(x):
    high = x.astype(BF16)
    return high, (x - high.astype(F32)).astype(BF16)


def one_hot(mask):
    return jnp.where(mask, 1.0, 0.0).astype(BF16)


def prepare_kernel(fan, nbr_ref, ends_ref, count_ref, table_ref, pairs_ref, degree_ref):
    nodes, slots = table_ref.shape[1:]
    step = 64

    @pl.loop(0, nodes // step)
    def _(block):
        rows = pl.ds(pl.multiple_of(block * step, step), step)
        lanes = lax.broadcasted_iota(jnp.int32, (step, slots), 1)
        named = nbr_ref[rows, :]
        for relation in range(table_ref.shape[0]):
            total = jnp.zeros((step, slots), F32)
            for k in range(fan):
                column = relation * fan + k
                total = total + jnp.where(named[:, column : column + 1] == lanes, 1.0, 0.0)
            table_ref[relation, rows, :] = total.astype(BF16)

    pairs_ref[...] = jnp.zeros_like(pairs_ref)

    @pl.loop(0, count_ref[0])
    def _(tile):
        ends = ends_ref[tile]
        rows = lax.broadcasted_iota(jnp.int32, (nodes, ends.shape[1]), 0)
        pairs_ref[...] += nt(one_hot(ends[0:1, :] == rows), one_hot(ends[1:2, :] == rows))

    pairs = pairs_ref[...]
    degree_ref[...] = jnp.sum(pairs, axis=1, keepdims=True)
    pairs_ref[...] = pairs + pairs.T


def layer_kernel(fan, own_ref, halo_ref, weights_ref, table_ref, ids_ref, means_ref, embed_ref, neg_ref):
    nodes = own_ref.shape[0]
    own = own_ref[...]
    preact = nn(own, weights_ref[0])
    for relation in range(table_ref.shape[0]):
        total = nn(table_ref[relation, :, :nodes], own) + nn(table_ref[relation, :, nodes:], halo_ref[...])
        mean = (total / fan).astype(BF16)
        means_ref[relation] = mean
        preact = preact + nn(mean, weights_ref[relation + 1])
    embedding = preact.astype(BF16)
    embed_ref[...] = embedding
    lanes = lax.broadcasted_iota(jnp.int32, (ids_ref.shape[0], nodes), 1)
    neg_ref[...] = nn(one_hot(ids_ref[...] == lanes), embedding).astype(BF16)


def positive_kernel(embed_ref, pairs_ref, grad_ref, loss_ref):
    embedding = embed_ref[...]
    pairs = pairs_ref[...]
    score = nt(embedding, embedding)
    small = jnp.exp(-jnp.abs(score))
    loss = jnp.maximum(-score, 0.0) + jnp.log1p(small)
    loss_ref[...] = 0.5 * jnp.sum(pairs * loss, axis=0, keepdims=True)
    high, low = halves(-pairs * (jnp.where(score >= 0, small, 1.0) / (1.0 + small)))
    grad_ref[...] = nn(high, embedding) + nn(low, embedding)


def negative_kernel(embed_ref, negs_ref, degree_ref, positive_ref, grad_ref, neg_grad_ref, loss_ref):
    embedding = embed_ref[...]
    negatives = negs_ref[...]
    degree = degree_ref[...]
    count = negatives.shape[0]
    score = nt(embedding, negatives)
    small = jnp.exp(-jnp.abs(score))
    loss = jnp.maximum(score, 0.0) + jnp.log1p(small)
    loss_ref[...] = jnp.sum(degree * loss, axis=0, keepdims=True) / count
    slope = ((jnp.where(score >= 0, 1.0, small) / (1.0 + small)) / count).astype(BF16)
    grad_ref[...] = positive_ref[...] + degree * nn(slope, negatives)
    high, low = halves(degree * embedding.astype(F32))
    neg_grad_ref[...] = tn(slope, high) + tn(slope, low)


def gradient_kernel(own_ref, means_ref, grad_ref, neg_parts_ref, ids_ref, pre_ref, terms_ref):
    nodes = grad_ref.shape[0]
    total = neg_parts_ref[0]
    for part in range(1, neg_parts_ref.shape[0]):
        total = total + neg_parts_ref[part]
    rows = lax.broadcasted_iota(jnp.int32, (nodes, 1), 0)
    grad = grad_ref[...]
    for j in range(total.shape[0]):
        grad = grad + jnp.where(ids_ref[j : j + 1, :] == rows, total[j : j + 1, :], 0.0)
    pre = grad.astype(BF16)
    pre_ref[...] = pre
    terms_ref[0] = tn(own_ref[...], pre)
    for relation in range(means_ref.shape[0]):
        terms_ref[relation + 1] = tn(means_ref[relation], pre)


def call(kernel, out_shape, in_specs, **kwargs):
    many = isinstance(out_shape, (list, tuple))
    return pl.pallas_call(
        kernel,
        out_shape=out_shape,
        in_specs=in_specs,
        out_specs=whole(len(out_shape)) if many else whole(1)[0],
        compiler_params=pltpu.CompilerParams(vmem_limit_bytes=VMEM_LIMIT),
        **kwargs,
    )


def shape(dims, kind):
    return jax.ShapeDtypeStruct(dims, kind)


def on_device(parts, features, weights, halo_send, nbr_index, tile_count, edge_ends, neg_ids):
    nodes, width = features.shape
    relations, fan = nbr_index.shape[1:]
    per_peer = halo_send.shape[2]
    slots = nodes + parts * per_peer
    own_neg = neg_ids.shape[0]
    count_neg = own_neg * parts
    wanted = halo_send.reshape(-1, 1)
    columns = lax.broadcasted_iota(jnp.int32, (parts * per_peer, nodes), 1)
    outgoing = nn((wanted == columns).astype(BF16), features).astype(BF16)
    incoming = lax.all_to_all(
        outgoing.reshape(parts, per_peer, width), "dom", split_axis=0, concat_axis=0, tiled=True
    ).reshape(-1, width)
    table, pairs, degree = call(
        functools.partial(prepare_kernel, fan),
        (
            shape((relations, nodes, slots), BF16),
            shape((nodes, nodes), F32),
            shape((nodes, 1), F32),
        ),
        whole(2) + [pl.BlockSpec(memory_space=pltpu.SMEM)],
    )(nbr_index.reshape(nodes, relations * fan), edge_ends, tile_count)
    ids = neg_ids.reshape(-1, 1)
    means, embedding, my_negs = call(
        functools.partial(layer_kernel, fan),
        (
            shape((relations, nodes, width), BF16),
            shape((nodes, width), BF16),
            shape((own_neg, width), BF16),
        ),
        whole(5),
    )(features, incoming, weights, table, ids)
    negatives = lax.all_to_all(
        jnp.broadcast_to(my_negs[None], (parts, own_neg, width)), "dom", split_axis=0, concat_axis=0, tiled=True
    ).reshape(count_neg, width)
    positive_grad, loss_a = call(
        positive_kernel, (shape((nodes, width), F32), shape((1, nodes), F32)), whole(2)
    )(embedding, pairs)
    node_grad, neg_grad, loss_b = call(
        negative_kernel,
        (shape((nodes, width), F32), shape((count_neg, width), F32), shape((1, count_neg), F32)),
        whole(4),
    )(embedding, negatives, degree, positive_grad)
    neg_parts = lax.all_to_all(
        neg_grad.reshape(parts, own_neg, width), "dom", split_axis=0, concat_axis=0, tiled=True
    )
    pre_grad, terms = call(
        gradient_kernel,
        (shape((nodes, width), BF16), shape((relations + 1, width, width), F32)),
        whole(5),
    )(features, means, node_grad, neg_parts, ids)
    loss = jnp.sum(loss_a) + jnp.sum(loss_b)
    edges = tile_count[0].astype(F32) * edge_ends.shape[2]
    weight_sum, total_loss, edge_total = lax.psum((terms, loss, edges), "dom")
    return (weight_sum / edge_total, total_loss / edge_total, pre_grad)


def solution(mesh):
    placed = (
        P("dom", None),
        P(),
        P("dom", None, None),
        P("dom", None, None),
        P("dom"),
        P("dom", None, None),
        P("dom"),
    )
    return jax.shard_map(
        functools.partial(on_device, mesh.shape["dom"]),
        mesh=mesh,
        in_specs=placed,
        out_specs=(P(), P(), P("dom", None)),
        check_vma=False,
    )
```

time: 580 us -> 229 us (0.39)
  waiting for transfers between devices: 280 us -> 101 us
  local copies, waits for them, and re-layouts: 84.1 us -> 13.1 us
  other arithmetic: 59.4 us -> 5.92 us
  blocking collectives: 85.9 us -> 57.8 us
  matrix products: 28.4 us -> 1.32 us
  Pallas kernels: 0 us -> 12.4 us
  loops' own time: 10.2 us -> 0 us
  starting transfers between devices: 11.3 us -> 18.1 us
    reduce_scatter x1 -> x0, waiting for transfers between devices: 166 us -> none  [on_device(): lax.psum_scatter(neg_grad, 'dom', scatter_dimension=0, tiled=True)]
    gather x33 -> x0, local copies, waits for them, and re-layouts: 76.9 us -> none  [the longest x16 40 us: neighbour_mean(): lookup[neighbours[:, column]].astype(jnp.float32)]
    all_gather x1 -> x0, blocking collectives: 47.8 us -> none  [on_device(): negatives = lax.all_gather(embedding[neg_ids], 'dom', axis=0, tiled=True)]
    scatter-add x15 -> x0, other arithmetic: 36.7 us -> none  [the longest x14 35.5 us: score_local(): node_grad.at[pair_ends[0]].add(source_grad).at[pair_ends[1]]]
    dot_general x27 -> x1, matrix products: 28.4 us -> 1.32 us  [nn(): return jnp.dot(a, b, preferred_element_type=F32)]
    all_to_all x0 -> x1, blocking collectives: none -> 17.8 us  [on_device(): lax.all_to_all(neg_grad.reshape(parts, own_neg, width), 'dom', split_axis...]
    ppermute x4 -> x0, waiting for transfers between devices: 15.7 us -> none  [swapped(): lax.ppermute(x, axis, [(i, i ^ 1 << bit) for i in range(lax.axis_size(axi...]
    pallas_call x0 -> x5, Pallas kernels: none -> 12.4 us  [the longest x1 3.9 us: on_device(): call(functools.partial(prepare_kernel, fan), (shape((relations, nodes, sl...]
  transfers between devices with their start and end apart: 7 -> 3, of which waited for: 4 -> 2; matrix products, arithmetic and copies ran while one was open for 28% -> 1% of each run, Pallas kernels for 0% -> 2%
where the time goes in v1:
time: 229 us; the launch traced here: 228 us
  waiting for transfers between devices  101 us (44%)
  blocking collectives  57.8 us (25%)
  between operations  18.5 us (8%)
  starting transfers between devices  18.1 us (8%)
  local copies, waits for them, and re-layouts  13.1 us (6%)
  Pallas kernels  12.4 us (5%)
  other arithmetic  5.92 us (3%)
    psum x1, waiting for transfers between devices, on_device(): weight_sum, total_loss, edge_total = lax.psum((terms, loss, edges), 'dom')  93.4 us
    psum x1, blocking collectives, on_device(): weight_sum, total_loss, edge_total = lax.psum((terms, loss, edges), 'dom')  40 us
    all_to_all x1, blocking collectives, on_device(): lax.all_to_all(neg_grad.reshape(parts, own_neg, width), 'dom', split_axis...  17.8 us
    all_to_all x1, starting transfers between devices, on_device(): lax.all_to_all(jnp.broadcast_to(my_negs[None], (parts, own_neg, width)),...  10.7 us
    unnamed x25, local copies, waits for them, and re-layouts  9.88 us
    all_to_all x1, waiting for transfers between devices, on_device(): lax.all_to_all(jnp.broadcast_to(my_negs[None], (parts, own_neg, width)),...  7.51 us
    all_to_all x1, starting transfers between devices, on_device(): lax.all_to_all(outgoing.reshape(parts, per_peer, width), 'dom', split_axi...  7.33 us
    div x1, other arithmetic, on_device(): return (weight_sum / edge_total, total_loss / edge_total, pre_grad)  4.64 us
  transfers between devices with their start and end apart: 3, of which 2 were waited for; matrix products, arithmetic and copies ran while one was open for 1% of the time, Pallas kernels for 2%

profile of v1, /device:TPU:0, one launch (start us, length us, event | category | flops | bytes accessed | tf_op | source)
XLA Modules:
  0.0 228.0 jit_solution(10536415501514148967)
XLA Ops:
  7.2 0.0 copy-start.2
  7.2 0.9 copy.14
  8.1 0.1 eq.10
  8.2 1.3 convolution_convert_fusion
  9.5 0.7 reshape.30
  10.2 7.3 %all-to-all-start = ((bf16[32,4,512]{2,1,0:T(4,128)(2,1)}), bf16[32,4,512]{2,1,0:T(4,128)(2,1)S(1)}, u32[]{:S(2)}, u32[]{:S(2)}) async-start(bf16[32,4,512]{2,1,0:T(4,128)(2,1)} %reshape.30), calls=%async_computation | async-start | bytes 262144 | tf_op jit(solution)/shard_map/all_to_all | solution.py:152
  18.2 0.7 copy.16.ids_ref
  18.9 0.9 copy.15.nbr_ref
  19.8 0.0 copy-start.11
  19.8 0.8 copy-done.11
  20.5 3.9 %shard_map.94 = (bf16[2,512,640]{2,1,0:T(8,128)(2,1)S(1)}, f32[512,512]{1,0:T(8,128)S(1)}, f32[512,1]{1,0:T(8,128)S(1)}) custom-call(s32[512,16]{1,0:T(8,128)S(1)} %copy.15.nbr_ref, s32[16,2,256]{2,1,0:T(2,128)S(1)} %copy-done.11, s32[1]{0:T(128)S(6)} %copy.19.count_ref), custom_call_target="tpu_custom_call" | custom-call | tf_op jit(solution)/shard_map/pallas_call | solution.py:155
  24.4 0.0 copy-start.3
  24.5 1.0 copy-done.3
  25.5 0.0 copy-start.5
  25.5 1.0 copy-done.5
  26.5 0.0 copy-start.9
  26.5 0.7 copy-done.9
  27.2 0.0 all-to-all-done
  27.2 0.0 copy-done.2
  27.2 0.0 copy-start
  27.3 1.0 copy-done
  28.3 0.0 copy-start.4
  28.3 1.3 copy-done.4
  29.6 1.9 shard_map.95
  31.5 0.0 copy-start.7
  31.5 1.0 copy-done.7
  32.5 0.0 copy-start.1
  32.5 0.7 broadcast_in_dim.2
  33.2 10.7 %all-to-all-start.1 = ((bf16[32,8,512]{2,1,0:T(8,128)(2,1)}), bf16[32,8,512]{2,1,0:T(8,128)(2,1)S(1)}, u32[]{:S(2)}, u32[]{:S(2)}) async-start(bf16[32,8,512]{2,1,0:T(8,128)(2,1)} %broadcast_in_dim.2), calls=%async_computation.1 | async-start | bytes 524288 | tf_op jit(solution)/shard_map/all_to_all | solution.py:174
  43.9 0.0 all-reduce.3.cloned.1.call-start
  44.0 0.0 copy-start.6
  44.0 1.2 copy-done.6
  45.2 0.0 copy-start.8
  45.2 1.8 shard_map.96
  47.0 7.5 %all-to-all-done.1 = bf16[32,8,512]{2,1,0:T(8,128)(2,1)S(1)} async-done(((bf16[32,8,512]{2,1,0:T(8,128)(2,1)}), bf16[32,8,512]{2,1,0:T(8,128)(2,1)S(1)}, u32[]{:S(2)}, u32[]{:S(2)}) %all-to-all-start.1) | async-done | bytes 262176 | tf_op jit(solution)/shard_map/all_to_all | solution.py:174
  54.5 0.0 copy-start.10
  54.5 0.9 copy-done.10
  55.5 1.4 shard_map.97
  56.8 17.8 %all_to_all.15.neg_parts_ref = f32[32,8,512]{2,1,0:T(8,128)S(1)} all-to-all(f32[32,8,512]{2,1,0:T(8,128)S(1)} %bitcast.7), channel_id=1, replica_groups=mesh['dom'=32] {'dom'}, dimensions={0} | all-to-all | bytes 1048576 | tf_op jit(solution)/shard_map/all_to_all | solution.py:185
  74.7 0.0 copy-done.1
  74.7 0.0 copy-done.8
  74.7 3.5 %shard_map.98 = (bf16[512,512]{1,0:T(8,128)(2,1)}, f32[3,512,512]{2,1,0:T(8,128)}) custom-call(bf16[512,512]{1,0:T(8,128)(2,1)S(1)} %copy-done.1, bf16[2,512,512]{2,1,0:T(8,128)(2,1)S(1)} %copy-done.8, f32[512,512]{1,0:T(8,128)S(1)} %get-tuple-element.23.grad_ref, f32[32,8,512]{2,1,0:T(8,128)S(1)} %all_to_all.15.neg_parts_ref, s32[8,1]{1,0:T(8,128)S(1)} %copy.16.ids_ref), custom_call_target="tpu_custom_call" | custom-call | tf_op jit(solution)/shard_map/pallas_call | solution.py:188
  78.1 0.0 all-reduce.3.cloned.1.call-update
  78.2 0.6 reduce_sum.18
  78.8 0.7 reduce_sum.19
  80.7 40.0 %all-reduce = (f32[]{:T(128)}, f32[]{:T(128)}) all-reduce(f32[]{:T(128)} %bitcast.4, f32[]{:T(128)S(6)} %add.9), channel_id=1, replica_groups=mesh['dom'=32] {'dom'}, use_global_device_ids=true, to_apply=%region_1.0 | all-reduce | flops 2 | bytes 16 | tf_op jit(solution)/shard_map/psum | solution.py:195
  122.0 93.4 %all-reduce.3.cloned.1.call-done = f32[3,512,512]{2,1,0:T(8,128)} async-done(((f32[3,512,512]{2,1,0:T(8,128)}), f32[3,512,512]{2,1,0:T(8,128)}) %all-reduce.3.cloned.1.call-update) | async-done | bytes 3145744 | tf_op jit(solution)/shard_map/psum | solution.py:195
  215.4 4.6 %broadcast_divide_fusion = f32[3,512,512]{2,1,0:T(8,128)} fusion(f32[3,512,512]{2,1,0:T(8,128)} %all-reduce.3.cloned.1.call-done, f32[]{:T(128)} %get-tuple-element.29), kind=kLoop, calls=%fused_computation | loop fusion | flops 786432 | bytes 6291460 | tf_op jit(solution)/shard_map/div | solution.py:196
  (1 shorter events, 0.0 us)
Async XLA Ops:
  7.2 20.1 %copy-start.2 = (bf16[3,512,512]{2,1,0:T(8,128)(2,1)S(1)}, bf16[3,512,512]{2,1,0:T(8,128)(2,1)}, u32[]{:S(2)}) copy-start(bf16[3,512,512]{2,1,0:T(8,128)(2,1)} %weights_ref.1) | copy-start | bytes 4718596
  10.2 17.0 %all-to-all-start = ((bf16[32,4,512]{2,1,0:T(4,128)(2,1)}), bf16[32,4,512]{2,1,0:T(4,128)(2,1)S(1)}, u32[]{:S(2)}, u32[]{:S(2)}) async-start(bf16[32,4,512]{2,1,0:T(4,128)(2,1)} %reshape.30), calls=%async_computation | async-start | bytes 262144 | tf_op jit(solution)/shard_map/all_to_all | solution.py:152
  19.8 0.8 copy-start.11
  24.4 1.1 copy-start.3
  25.5 1.0 copy-start.5
  26.5 0.7 copy-start.9
  27.2 1.0 copy-start
  28.3 1.3 copy-start.4
  31.5 1.0 copy-start.7
  32.5 42.2 %copy-start.1 = (bf16[512,512]{1,0:T(8,128)(2,1)S(1)}, bf16[512,512]{1,0:T(8,128)(2,1)}, u32[]{:S(2)}) copy-start(bf16[512,512]{1,0:T(8,128)(2,1)} %own_ref.3) | copy-start | bytes 1572868
  33.2 21.3 %all-to-all-start.1 = ((bf16[32,8,512]{2,1,0:T(8,128)(2,1)}), bf16[32,8,512]{2,1,0:T(8,128)(2,1)S(1)}, u32[]{:S(2)}, u32[]{:S(2)}) async-start(bf16[32,8,512]{2,1,0:T(8,128)(2,1)} %broadcast_in_dim.2), calls=%async_computation.1 | async-start | bytes 524288 | tf_op jit(solution)/shard_map/all_to_all | solution.py:174
  43.9 171.5 %all-reduce.3.cloned.1.call-start = ((), (), s32[]{:S(2)}) async-start(), calls=%async_computation.3 | async-start | bytes 6291456 | tf_op jit(solution)/shard_map/psum | solution.py:195
  44.0 1.2 copy-start.6
  45.2 29.4 %copy-start.8 = (bf16[2,512,512]{2,1,0:T(8,128)(2,1)S(1)}, bf16[2,512,512]{2,1,0:T(8,128)(2,1)}, u32[]{:S(2)}) copy-start(bf16[2,512,512]{2,1,0:T(8,128)(2,1)} %copy-done.7) | copy-start | bytes 3145732
  54.5 1.0 copy-start.10
Sparse Core Ops, SparseCore 0:
  78.3 137.0 all-reduce.2

commit v2 on v1

--- a/solution.py
+++ b/solution.py
@@ -10,6 +10,8 @@
 F32 = jnp.float32
 BF16 = jnp.bfloat16
 VMEM_LIMIT = 48 * 1024 * 1024
+LANES = 128
+MESH = pl.DeviceIdType.MESH
 
 
 def whole(count):
@@ -92,45 +94,223 @@
     grad_ref[...] = nn(high, embedding) + nn(low, embedding)
 
 
-def negative_kernel(embed_ref, negs_ref, degree_ref, positive_ref, grad_ref, neg_grad_ref, loss_ref):
+def negative_kernel(embed_ref, negs_ref, degree_ref, positive_ref, loss_ref, count_ref, edge_ref, grad_ref, send_ref):
+    parts, own_neg, _ = send_ref.shape
     embedding = embed_ref[...]
+    width = embedding.shape[1]
     negatives = negs_ref[...]
     degree = degree_ref[...]
     count = negatives.shape[0]
     score = nt(embedding, negatives)
     small = jnp.exp(-jnp.abs(score))
     loss = jnp.maximum(score, 0.0) + jnp.log1p(small)
-    loss_ref[...] = jnp.sum(degree * loss, axis=0, keepdims=True) / count
+    loss_sum = jnp.sum(loss_ref[...]) + jnp.sum(degree * loss) / count
     slope = ((jnp.where(score >= 0, 1.0, small) / (1.0 + small)) / count).astype(BF16)
     grad_ref[...] = positive_ref[...] + degree * nn(slope, negatives)
     high, low = halves(degree * embedding.astype(F32))
-    neg_grad_ref[...] = tn(slope, high) + tn(slope, low)
-
-
-def gradient_kernel(own_ref, means_ref, grad_ref, neg_parts_ref, ids_ref, pre_ref, terms_ref):
-    nodes = grad_ref.shape[0]
-    total = neg_parts_ref[0]
-    for part in range(1, neg_parts_ref.shape[0]):
-        total = total + neg_parts_ref[part]
+    neg_grad = tn(slope, high) + tn(slope, low)
+    send_ref[:, :, :width] = neg_grad.reshape(parts, own_neg, width)
+    edges = count_ref[0].astype(F32) * edge_ref.shape[1]
+    rows = lax.broadcasted_iota(jnp.int32, (own_neg, LANES), 0)
+    tile = jnp.where(rows == 0, loss_sum, edges)
+    send_ref[:, :, width:] = jnp.broadcast_to(tile[None], (parts, own_neg, LANES))
+
+
+def greet(peers):
+    barrier = pltpu.get_barrier_semaphore()
+    for peer in peers:
+        pl.semaphore_signal(barrier, inc=1, device_id=(peer,), device_id_type=MESH)
+    pl.semaphore_wait(barrier, len(peers))
+
+
+def exchange_kernel(parts, send_ref, total_ref, landed, send_sem, recv_sem):
+    me = lax.axis_index("dom")
+    barrier = pltpu.get_barrier_semaphore()
+
+    def copy_to(peer, slot, sem):
+        return pltpu.make_async_remote_copy(
+            src_ref=send_ref.at[peer],
+            dst_ref=landed.at[slot],
+            send_sem=send_sem.at[sem],
+            recv_sem=recv_sem.at[slot],
+            device_id=(peer,),
+            device_id_type=MESH,
+        )
+
+    @pl.loop(1, parts)
+    def _(i):
+        pl.semaphore_signal(barrier, inc=1, device_id=((me + i) % parts,), device_id_type=MESH)
+
+    pl.semaphore_wait(barrier, parts - 1)
+
+    @pl.loop(1, parts)
+    def _(i):
+        copy_to((me + i) % parts, me, i).start()
+
+    landed[me] = send_ref[me]
+
+    @pl.loop(1, parts)
+    def _(i):
+        copy_to((me + i) % parts, (me + i) % parts, i).wait()
+
+    total = landed[0]
+    for part in range(1, parts):
+        total = total + landed[part]
+    total_ref[...] = total
+
+
+def reduce_plan(parts, colors):
+    radix = [1, 1, 1]
+    at = 0
+    while radix[0] * radix[1] * radix[2] * 2 < parts:
+        radix[at % 3] *= 2
+        at += 1
+    outer, middle, inner = radix
+    core = (2, 1)
+    dims = [(inner, 2), (middle, 2 * inner), (outer, 2 * inner * middle)]
+    return [[core] + [dims[(color + k) % 3] for k in range(3)] for color in range(colors)]
+
+
+def reduce_kernel(plan, terms_ref, edges_ref, out_ref, *scratch):
+    colors = len(plan)
+    phases = len(plan[0])
+    me = lax.axis_index("dom")
+    landed = [scratch[color * phases : (color + 1) * phases] for color in range(colors)]
+    scratch = scratch[colors * phases :]
+    sums = [scratch[color * phases : (color + 1) * phases] for color in range(colors)]
+    send_sem, recv_sem = scratch[colors * phases :]
+    spots = {}
+
+    def spot(*key):
+        return spots.setdefault(key, len(spots))
+
+    def place(color, phase):
+        size, stride = plan[color][phase]
+        return size, stride, (me // stride) % size
+
+    def remote(source, target, key, peer):
+        at = spot(*key)
+        return pltpu.make_async_remote_copy(
+            src_ref=source,
+            dst_ref=target,
+            send_sem=send_sem.at[at],
+            recv_sem=recv_sem.at[at],
+            device_id=(peer,),
+            device_id_type=MESH,
+        )
+
+    greet([
+        me + ((me // stride + delta) % size - (me // stride) % size) * stride
+        for size, stride in plan[0]
+        for delta in range(1, size)
+    ])
+
+    def scatter_copies(color, phase):
+        size, stride, mine = place(color, phase)
+        source = terms_ref.at[color] if phase == 0 else sums[color][phase - 1]
+        length = source.shape[0] // size
+        copies = []
+        for delta in range(1, size):
+            other = (mine + delta) % size
+            copies.append(
+                remote(
+                    source.at[pl.ds(other * length, length)],
+                    landed[color][phase].at[delta - 1],
+                    ("scatter", color, phase, delta),
+                    me + (other - mine) * stride,
+                )
+            )
+        return copies
+
+    def regions(color):
+        off, length = 0, terms_ref.shape[1]
+        found = [(off, length)]
+        for phase in range(phases):
+            size, _, mine = place(color, phase)
+            length = length // size
+            off = off + mine * length
+            found.append((off, length))
+        return found
+
+    def gather_copies(color, phase):
+        size, stride, mine = place(color, phase)
+        off, length = regions(color)[phase + 1]
+        block = out_ref.at[color, pl.ds(off, length)]
+        return [
+            remote(block, block, ("gather", color, phase, delta), me + ((mine + delta) % size - mine) * stride)
+            for delta in range(1, size)
+        ]
+
+    flying = [scatter_copies(color, 0) for color in range(colors)]
+    for copies in flying:
+        for copy in copies:
+            copy.start()
+    for phase in range(phases):
+        for color in range(colors):
+            for copy in flying[color]:
+                copy.wait()
+            size, _, mine = place(color, phase)
+            source = terms_ref.at[color] if phase == 0 else sums[color][phase - 1]
+            length = source.shape[0] // size
+            total = source[pl.ds(mine * length, length)]
+            for slot in range(size - 1):
+                total = total + landed[color][phase][slot]
+            if phase < phases - 1:
+                sums[color][phase][...] = total
+                flying[color] = scatter_copies(color, phase + 1)
+            else:
+                off, length = regions(color)[phases]
+                out_ref[color, pl.ds(off, length)] = total / edges_ref[...][None]
+                flying[color] = gather_copies(color, phase)
+            for copy in flying[color]:
+                copy.start()
+    for phase in reversed(range(phases)):
+        for color in range(colors):
+            for copy in flying[color]:
+                copy.wait()
+            if phase > 0:
+                flying[color] = gather_copies(color, phase - 1)
+                for copy in flying[color]:
+                    copy.start()
+
+
+def gradient_kernel(own_ref, means_ref, grad_ref, total_ref, ids_ref, pre_ref, terms_ref, edges_ref, loss_ref):
+    nodes, width = grad_ref.shape
+    total = total_ref[...]
     rows = lax.broadcasted_iota(jnp.int32, (nodes, 1), 0)
     grad = grad_ref[...]
     for j in range(total.shape[0]):
-        grad = grad + jnp.where(ids_ref[j : j + 1, :] == rows, total[j : j + 1, :], 0.0)
+        grad = grad + jnp.where(ids_ref[j : j + 1, :] == rows, total[j : j + 1, :width], 0.0)
     pre = grad.astype(BF16)
     pre_ref[...] = pre
-    terms_ref[0] = tn(own_ref[...], pre)
-    for relation in range(means_ref.shape[0]):
-        terms_ref[relation + 1] = tn(means_ref[relation], pre)
-
-
-def call(kernel, out_shape, in_specs, **kwargs):
+    tall = width // 8
+    for term in range(terms_ref.shape[0]):
+        left = own_ref[...] if term == 0 else means_ref[term - 1]
+        product = tn(left, pre)
+        for j in range(width // LANES):
+            terms_ref[term, j * tall : (j + 1) * tall] = product[:, j * LANES : (j + 1) * LANES].reshape(tall, 8, LANES)
+    edges = total[1:2, width:]
+    edges_ref[...] = jnp.broadcast_to(edges, edges_ref.shape)
+    loss_ref[...] = total[0:1, width:] / edges
+
+
+def finish_kernel(tiles_ref, out_ref):
+    width = out_ref.shape[2]
+    tall = width // 8
+    for term in range(out_ref.shape[0]):
+        for j in range(width // LANES):
+            out_ref[term, :, j * LANES : (j + 1) * LANES] = tiles_ref[term, j * tall : (j + 1) * tall].reshape(width, LANES)
+
+
+def call(kernel, out_shape, in_specs, collective=None, **kwargs):
+    extra = {} if collective is None else {"collective_id": collective, "has_side_effects": True}
     many = isinstance(out_shape, (list, tuple))
     return pl.pallas_call(
         kernel,
         out_shape=out_shape,
         in_specs=in_specs,
         out_specs=whole(len(out_shape)) if many else whole(1)[0],
-        compiler_params=pltpu.CompilerParams(vmem_limit_bytes=VMEM_LIMIT),
+        compiler_params=pltpu.CompilerParams(vmem_limit_bytes=VMEM_LIMIT, **extra),
         **kwargs,
     )
 
@@ -177,23 +357,46 @@
     positive_grad, loss_a = call(
         positive_kernel, (shape((nodes, width), F32), shape((1, nodes), F32)), whole(2)
     )(embedding, pairs)
-    node_grad, neg_grad, loss_b = call(
+    node_grad, outbound = call(
         negative_kernel,
-        (shape((nodes, width), F32), shape((count_neg, width), F32), shape((1, count_neg), F32)),
-        whole(4),
-    )(embedding, negatives, degree, positive_grad)
-    neg_parts = lax.all_to_all(
-        neg_grad.reshape(parts, own_neg, width), "dom", split_axis=0, concat_axis=0, tiled=True
-    )
-    pre_grad, terms = call(
+        (shape((nodes, width), F32), shape((parts, own_neg, width + LANES), F32)),
+        whole(5) + [pl.BlockSpec(memory_space=pltpu.SMEM), pl.BlockSpec(memory_space=pltpu.VMEM)],
+    )(embedding, negatives, degree, positive_grad, loss_a, tile_count, edge_ends[0])
+    total = call(
+        functools.partial(exchange_kernel, parts),
+        shape((own_neg, width + LANES), F32),
+        whole(1),
+        collective=1,
+        scratch_shapes=[
+            pltpu.VMEM(outbound.shape, F32),
+            pltpu.SemaphoreType.DMA((parts,)),
+            pltpu.SemaphoreType.DMA((parts,)),
+        ],
+    )(outbound)
+    tiles = (relations + 1, width * width // (8 * LANES), 8, LANES)
+    pre_grad, terms, edges, loss = call(
         gradient_kernel,
-        (shape((nodes, width), BF16), shape((relations + 1, width, width), F32)),
+        (shape((nodes, width), BF16), shape(tiles, F32), shape((8, LANES), F32), shape((1, LANES), F32)),
         whole(5),
-    )(features, means, node_grad, neg_parts, ids)
-    loss = jnp.sum(loss_a) + jnp.sum(loss_b)
-    edges = tile_count[0].astype(F32) * edge_ends.shape[2]
-    weight_sum, total_loss, edge_total = lax.psum((terms, loss, edges), "dom")
-    return (weight_sum / edge_total, total_loss / edge_total, pre_grad)
+    )(features, means, node_grad, total, ids)
+    plan = reduce_plan(parts, tiles[0])
+    landed, sums, copies = [], [], 0
+    for dims in plan:
+        length = tiles[1]
+        for size, _ in dims:
+            length = length // size
+            landed.append(pltpu.VMEM((size - 1, length, 8, LANES), F32))
+            sums.append(pltpu.VMEM((length, 8, LANES), F32))
+            copies += 2 * (size - 1)
+    reduced = call(
+        functools.partial(reduce_kernel, plan),
+        shape(tiles, F32),
+        whole(2),
+        collective=2,
+        scratch_shapes=landed + sums + [pltpu.SemaphoreType.DMA((copies,)), pltpu.SemaphoreType.DMA((copies,))],
+    )(terms, edges)
+    weight_grad = call(finish_kernel, shape((relations + 1, width, width), F32), whole(1))(reduced)
+    return (weight_grad, loss[0, 0], pre_grad)
 
 
 def solution(mesh):

time: 229 us -> 128 us (0.56)
  waiting for transfers between devices: 101 us -> 6.88 us
  Pallas kernels: 12.4 us -> 83.5 us
  blocking collectives: 57.8 us -> 0 us
  between operations: 18.5 us -> 1.42 us
  other arithmetic: 5.92 us -> 0 us
  local copies, waits for them, and re-layouts: 13.1 us -> 15.4 us
    psum x1 -> x0, waiting for transfers between devices: 93.4 us -> none  [on_device(): weight_sum, total_loss, edge_total = lax.psum((terms, loss, edges), 'dom')]
    pallas_call x2 -> x5, Pallas kernels: 4.84 us -> 76 us  [the longest x1 56.4 us: on_device(): call(functools.partial(reduce_kernel, plan), shape(tiles, F32), whole(2),...]
    psum x1 -> x0, blocking collectives: 40 us -> none  [on_device(): weight_sum, total_loss, edge_total = lax.psum((terms, loss, edges), 'dom')]
    all_to_all x1 -> x0, blocking collectives: 17.8 us -> none  [on_device(): lax.all_to_all(neg_grad.reshape(parts, own_neg, width), 'dom', split_axis...]
    div x1 -> x0, other arithmetic: 4.64 us -> none  [on_device(): return (weight_sum / edge_total, total_loss / edge_total, pre_grad)]
    unnamed x25 -> x27, local copies, waits for them, and re-layouts: 9.88 us -> 11.6 us
  transfers between devices with their start and end apart: 3 -> 2, of which waited for: 2 -> 1; matrix products, arithmetic and copies ran while one was open for 1% -> 2% of each run, Pallas kernels for 2% -> 4%
where the time goes in v2:
time: 128 us; the launch traced here: 127 us
  Pallas kernels  83.5 us (65%)
  starting transfers between devices  18.1 us (14%)
  local copies, waits for them, and re-layouts  15.4 us (12%)
  waiting for transfers between devices  6.88 us (5%)
  between operations  1.42 us (1%)
  matrix products  1.32 us (1%)
    pallas_call x1, Pallas kernels, on_device(): call(functools.partial(reduce_kernel, plan), shape(tiles, F32), whole(2),...  56.4 us
    pallas_call x1, Pallas kernels, on_device(): call(functools.partial(exchange_kernel, parts), shape((own_neg, width + L...  13.8 us
    unnamed x27, local copies, waits for them, and re-layouts  11.6 us
    all_to_all x1, starting transfers between devices, on_device(): lax.all_to_all(jnp.broadcast_to(my_negs[None], (parts, own_neg, width)),...  10.7 us
    all_to_all x1, starting transfers between devices, on_device(): lax.all_to_all(outgoing.reshape(parts, per_peer, width), 'dom', split_axi...  7.32 us
    all_to_all x1, waiting for transfers between devices, on_device(): lax.all_to_all(jnp.broadcast_to(my_negs[None], (parts, own_neg, width)),...  6.87 us
    pallas_call x1, Pallas kernels, on_device(): call(functools.partial(prepare_kernel, fan), (shape((relations, nodes, sl...  3.9 us
  transfers between devices with their start and end apart: 2, of which 1 were waited for; matrix products, arithmetic and copies ran while one was open for 2% of the time, Pallas kernels for 4%

profile of v2, /device:TPU:0, one launch (start us, length us, event | category | flops | bytes accessed | tf_op | source)
XLA Modules:
  0.0 126.6 jit_solution(4604460655379576530)
XLA Ops:
  0.6 0.0 copy-start.3
  0.6 0.9 copy.14
  1.5 0.1 eq.10
  1.6 1.3 %convolution_convert_fusion = bf16[128,512]{1,0:T(8,128)(2,1)S(1)} fusion(bf16[512,512]{1,0:T(8,128)(2,1)} %own_ref.3, s32[128]{0:T(128)S(1)} %eq.10), kind=kOutput, calls=%fused_computation | convolution fusion | flops 67239936 | bytes 655872 | tf_op jit(solution)/shard_map/dot_general | solution.py:22
  2.9 0.7 reshape.24
  3.6 7.3 %all-to-all-start = ((bf16[32,4,512]{2,1,0:T(4,128)(2,1)}), bf16[32,4,512]{2,1,0:T(4,128)(2,1)S(1)}, u32[]{:S(2)}, u32[]{:S(2)}) async-start(bf16[32,4,512]{2,1,0:T(4,128)(2,1)} %reshape.24), calls=%async_computation | async-start | bytes 262144 | tf_op jit(solution)/shard_map/all_to_all | solution.py:332
  11.6 0.7 copy.16.ids_ref
  12.4 0.9 copy.15.nbr_ref
  13.2 0.0 copy-start.12
  13.3 0.8 copy-done.12
  14.0 3.9 %shard_map.94 = (bf16[2,512,640]{2,1,0:T(8,128)(2,1)S(1)}, f32[512,512]{1,0:T(8,128)S(1)}, f32[512,1]{1,0:T(8,128)S(1)}) custom-call(s32[512,16]{1,0:T(8,128)S(1)} %copy.15.nbr_ref, s32[16,2,256]{2,1,0:T(2,128)S(1)} %copy-done.12, s32[1]{0:T(128)S(6)} %copy.18.count_ref), custom_call_target="tpu_custom_call" | custom-call | tf_op jit(solution)/shard_map/pallas_call | solution.py:335
  17.9 0.0 copy-start.4
  17.9 1.0 copy-done.4
  19.0 0.0 copy-start.6
  19.0 1.0 copy-done.6
  20.0 0.0 copy-start.10
  20.0 0.7 copy-done.10
  20.7 0.0 all-to-all-done
  20.7 0.0 copy-done.3
  20.7 0.0 copy-start
  20.7 1.0 copy-done
  21.8 0.0 copy-start.5
  21.8 1.3 %copy-done.5 = bf16[2,512,640]{2,1,0:T(8,128)(2,1)S(1)} copy-done((bf16[2,512,640]{2,1,0:T(8,128)(2,1)S(1)}, bf16[2,512,640]{2,1,0:T(8,128)(2,1)}, u32[]{:S(2)}) %copy-start.5) | copy-done | bytes 1310744
  23.1 1.9 %shard_map.95 = (bf16[2,512,512]{2,1,0:T(8,128)(2,1)S(1)}, bf16[512,512]{1,0:T(8,128)(2,1)S(1)}, bf16[8,512]{1,0:T(8,128)(2,1)S(1)}) custom-call(bf16[512,512]{1,0:T(8,128)(2,1)S(1)} %copy-done, bf16[128,512]{1,0:T(8,128)(2,1)S(1)} %reshape.25.halo_ref, bf16[3,512,512]{2,1,0:T(8,128)(2,1)S(1)} %copy-done.3, bf16[2,512,640]{2,1,0:T(8,128)(2,1)S(1)} %copy-done.5, ...), custom_call_target="tpu_custom_call" | custom-call | tf_op jit(solution)/shard_map/pallas_call | solution.py:345
  25.0 0.0 copy-start.8
  25.0 1.0 copy-done.8
  25.9 0.0 copy-start.1
  25.9 0.7 broadcast_in_dim.2
  26.7 10.7 %all-to-all-start.1 = ((bf16[32,8,512]{2,1,0:T(8,128)(2,1)}), bf16[32,8,512]{2,1,0:T(8,128)(2,1)S(1)}, u32[]{:S(2)}, u32[]{:S(2)}) async-start(bf16[32,8,512]{2,1,0:T(8,128)(2,1)} %broadcast_in_dim.2), calls=%async_computation.1 | async-start | bytes 524288 | tf_op jit(solution)/shard_map/all_to_all | solution.py:354
  37.4 0.7 slice_bitcast_fusion.edge_ref
  38.1 0.0 copy-start.7
  38.1 1.2 copy-done.7
  39.3 0.0 copy-start.9
  39.3 1.8 %shard_map.96 = (f32[512,512]{1,0:T(8,128)S(1)}, f32[1,512]{1,0:T(1,128)S(1)}) custom-call(bf16[512,512]{1,0:T(8,128)(2,1)S(1)} %get-tuple-element.19.embed_ref, f32[512,512]{1,0:T(8,128)S(1)} %copy-done.7), custom_call_target="tpu_custom_call" | custom-call | tf_op jit(solution)/shard_map/pallas_call | solution.py:357
  41.1 6.9 %all-to-all-done.1 = bf16[32,8,512]{2,1,0:T(8,128)(2,1)S(1)} async-done(((bf16[32,8,512]{2,1,0:T(8,128)(2,1)}), bf16[32,8,512]{2,1,0:T(8,128)(2,1)S(1)}, u32[]{:S(2)}, u32[]{:S(2)}) %all-to-all-start.1) | async-done | bytes 262176 | tf_op jit(solution)/shard_map/all_to_all | solution.py:354
  48.0 0.0 copy-start.11
  48.0 0.9 copy-done.11
  48.9 1.4 %shard_map.97 = (f32[512,512]{1,0:T(8,128)S(1)}, f32[32,8,640]{2,1,0:T(8,128)S(1)}) custom-call(bf16[512,512]{1,0:T(8,128)(2,1)S(1)} %get-tuple-element.19.embed_ref, bf16[256,512]{1,0:T(8,128)(2,1)S(1)} %bitcast.8, f32[512,1]{1,0:T(8,128)S(1)} %copy-done.11, f32[512,512]{1,0:T(8,128)S(1)} %get-tuple-element.23.positive_ref, ...), custom_call_target="tpu_custom_call" | custom-call | tf_op jit(solution)/shard_map/pallas_call | solution.py:360
  50.3 13.8 %shard_map.98.total_ref = f32[8,640]{1,0:T(8,128)S(1)} custom-call(f32[32,8,640]{2,1,0:T(8,128)S(1)} %get-tuple-element.26.send_ref), custom_call_target="tpu_custom_call" | custom-call | tf_op jit(solution)/shard_map/pallas_call | solution.py:365
  64.1 0.0 copy-done.1
  64.1 0.0 copy-done.9
  64.1 2.3 %shard_map.99 = (bf16[512,512]{1,0:T(8,128)(2,1)}, f32[3,256,8,128]{3,2,1,0:T(8,128)S(1)}, f32[8,128]{1,0:T(8,128)S(1)}, f32[1,128]{1,0:T(1,128)}) custom-call(bf16[512,512]{1,0:T(8,128)(2,1)S(1)} %copy-done.1, bf16[2,512,512]{2,1,0:T(8,128)(2,1)S(1)} %copy-done.9, f32[512,512]{1,0:T(8,128)S(1)} %get-tuple-element.25.grad_ref, ...), custom_call_target="tpu_custom_call" | custom-call | tf_op jit(solution)/shard_map/pallas_call | solution.py:377
  66.5 0.0 copy-start.2
  66.5 1.7 %copy-done.2 = f32[3,256,8,128]{3,2,1,0:T(8,128)} copy-done((f32[3,256,8,128]{3,2,1,0:T(8,128)}, f32[3,256,8,128]{3,2,1,0:T(8,128)S(1)}, u32[]{:S(2)}) %copy-start.2) | copy-done | bytes 3145752
  68.1 56.4 %shard_map.100.tiles_ref = f32[3,256,8,128]{3,2,1,0:T(8,128)S(1)} custom-call(f32[3,256,8,128]{3,2,1,0:T(8,128)} %copy-done.2, f32[8,128]{1,0:T(8,128)S(1)} %get-tuple-element.28.edges_ref), custom_call_target="tpu_custom_call" | custom-call | tf_op jit(solution)/shard_map/pallas_call | solution.py:391
  124.5 2.1 %shard_map.101 = f32[3,512,512]{2,1,0:T(8,128)} custom-call(f32[3,256,8,128]{3,2,1,0:T(8,128)S(1)} %shard_map.100.tiles_ref), custom_call_target="tpu_custom_call" | custom-call | tf_op jit(solution)/shard_map/pallas_call | solution.py:398
  (1 shorter events, 0.0 us)
Async XLA Ops:
  0.6 20.1 %copy-start.3 = (bf16[3,512,512]{2,1,0:T(8,128)(2,1)S(1)}, bf16[3,512,512]{2,1,0:T(8,128)(2,1)}, u32[]{:S(2)}) copy-start(bf16[3,512,512]{2,1,0:T(8,128)(2,1)} %weights_ref.1) | copy-start | bytes 4718596
  3.6 17.0 %all-to-all-start = ((bf16[32,4,512]{2,1,0:T(4,128)(2,1)}), bf16[32,4,512]{2,1,0:T(4,128)(2,1)S(1)}, u32[]{:S(2)}, u32[]{:S(2)}) async-start(bf16[32,4,512]{2,1,0:T(4,128)(2,1)} %reshape.24), calls=%async_computation | async-start | bytes 262144 | tf_op jit(solution)/shard_map/all_to_all | solution.py:332
  13.2 0.8 copy-start.12
  17.9 1.1 copy-start.4
  19.0 1.0 copy-start.6
  20.0 0.7 copy-start.10
  20.7 1.0 copy-start
  21.8 1.3 %copy-start.5 = (bf16[2,512,640]{2,1,0:T(8,128)(2,1)S(1)}, bf16[2,512,640]{2,1,0:T(8,128)(2,1)}, u32[]{:S(2)}) copy-start(bf16[2,512,640]{2,1,0:T(8,128)(2,1)} %copy-done.4) | copy-start | bytes 3932164
  25.0 1.0 copy-start.8
  25.9 38.2 %copy-start.1 = (bf16[512,512]{1,0:T(8,128)(2,1)S(1)}, bf16[512,512]{1,0:T(8,128)(2,1)}, u32[]{:S(2)}) copy-start(bf16[512,512]{1,0:T(8,128)(2,1)} %own_ref.3) | copy-start | bytes 1572868
  26.7 21.3 %all-to-all-start.1 = ((bf16[32,8,512]{2,1,0:T(8,128)(2,1)}), bf16[32,8,512]{2,1,0:T(8,128)(2,1)S(1)}, u32[]{:S(2)}, u32[]{:S(2)}) async-start(bf16[32,8,512]{2,1,0:T(8,128)(2,1)} %broadcast_in_dim.2), calls=%async_computation.1 | async-start | bytes 524288 | tf_op jit(solution)/shard_map/all_to_all | solution.py:354
  38.1 1.2 copy-start.7
  39.3 24.8 %copy-start.9 = (bf16[2,512,512]{2,1,0:T(8,128)(2,1)S(1)}, bf16[2,512,512]{2,1,0:T(8,128)(2,1)}, u32[]{:S(2)}) copy-start(bf16[2,512,512]{2,1,0:T(8,128)(2,1)} %copy-done.8) | copy-start | bytes 3145732
  48.0 1.0 copy-start.11
  66.5 1.7 %copy-start.2 = (f32[3,256,8,128]{3,2,1,0:T(8,128)}, f32[3,256,8,128]{3,2,1,0:T(8,128)S(1)}, u32[]{:S(2)}) copy-start(f32[3,256,8,128]{3,2,1,0:T(8,128)S(1)} %get-tuple-element.27.terms_ref) | copy-start | bytes 9437188

commit v3 on v2

--- a/solution.py
+++ b/solution.py
@@ -95,7 +95,7 @@
 
 
 def negative_kernel(embed_ref, negs_ref, degree_ref, positive_ref, loss_ref, count_ref, edge_ref, grad_ref, send_ref):
-    parts, own_neg, _ = send_ref.shape
+    _, chips, own_neg, _ = send_ref.shape
     embedding = embed_ref[...]
     width = embedding.shape[1]
     negatives = negs_ref[...]
@@ -109,11 +109,13 @@
     grad_ref[...] = positive_ref[...] + degree * nn(slope, negatives)
     high, low = halves(degree * embedding.astype(F32))
     neg_grad = tn(slope, high) + tn(slope, low)
-    send_ref[:, :, :width] = neg_grad.reshape(parts, own_neg, width)
+    blocks = neg_grad.reshape(chips, 2, own_neg, width)
+    for core in range(2):
+        send_ref[core, :, :, :width] = blocks[:, core]
     edges = count_ref[0].astype(F32) * edge_ref.shape[1]
     rows = lax.broadcasted_iota(jnp.int32, (own_neg, LANES), 0)
     tile = jnp.where(rows == 0, loss_sum, edges)
-    send_ref[:, :, width:] = jnp.broadcast_to(tile[None], (parts, own_neg, LANES))
+    send_ref[:, :, :, width:] = jnp.broadcast_to(tile[None, None], (2, chips, own_neg, LANES))
 
 
 def greet(peers):
@@ -123,39 +125,56 @@
     pl.semaphore_wait(barrier, len(peers))
 
 
-def exchange_kernel(parts, send_ref, total_ref, landed, send_sem, recv_sem):
+def exchange_kernel(parts, send_ref, total_ref, paired, chip, landed, pair_sem, send_sem, recv_sem):
     me = lax.axis_index("dom")
+    core = me % 2
+    place = me // 2
+    chips = parts // 2
     barrier = pltpu.get_barrier_semaphore()
-
-    def copy_to(peer, slot, sem):
+    partner = me + 1 - 2 * core
+
+    def copy_to(other, slot, sem):
         return pltpu.make_async_remote_copy(
-            src_ref=send_ref.at[peer],
+            src_ref=chip.at[other],
             dst_ref=landed.at[slot],
             send_sem=send_sem.at[sem],
             recv_sem=recv_sem.at[slot],
-            device_id=(peer,),
+            device_id=(2 * other + core,),
             device_id_type=MESH,
         )
 
-    @pl.loop(1, parts)
+    pl.semaphore_signal(barrier, inc=1, device_id=(partner,), device_id_type=MESH)
+
+    @pl.loop(1, chips)
     def _(i):
-        pl.semaphore_signal(barrier, inc=1, device_id=((me + i) % parts,), device_id_type=MESH)
-
-    pl.semaphore_wait(barrier, parts - 1)
-
-    @pl.loop(1, parts)
+        pl.semaphore_signal(barrier, inc=1, device_id=(2 * ((place + i) % chips) + core,), device_id_type=MESH)
+
+    pl.semaphore_wait(barrier, chips)
+    pair = pltpu.make_async_remote_copy(
+        src_ref=send_ref.at[1 - core],
+        dst_ref=paired,
+        send_sem=pair_sem.at[0],
+        recv_sem=pair_sem.at[1],
+        device_id=(partner,),
+        device_id_type=MESH,
+    )
+    pair.start()
+    pair.wait()
+    chip[...] = send_ref[core] + paired[...]
+
+    @pl.loop(1, chips)
     def _(i):
-        copy_to((me + i) % parts, me, i).start()
-
-    landed[me] = send_ref[me]
-
-    @pl.loop(1, parts)
+        copy_to((place + i) % chips, place, i).start()
+
+    landed[place] = chip[place]
+
+    @pl.loop(1, chips)
     def _(i):
-        copy_to((me + i) % parts, (me + i) % parts, i).wait()
+        copy_to((place + i) % chips, (place + i) % chips, i).wait()
 
     total = landed[0]
-    for part in range(1, parts):
-        total = total + landed[part]
+    for other in range(1, chips):
+        total = total + landed[other]
     total_ref[...] = total
 
 
@@ -166,9 +185,8 @@
         radix[at % 3] *= 2
         at += 1
     outer, middle, inner = radix
-    core = (2, 1)
-    dims = [(inner, 2), (middle, 2 * inner), (outer, 2 * inner * middle)]
-    return [[core] + [dims[(color + k) % 3] for k in range(3)] for color in range(colors)]
+    core, first, second, last = (2, 1), (inner, 2), (middle, 2 * inner), (outer, 2 * inner * middle)
+    return [[core, first, second, last] if color % 2 == 0 else [core, second, first, last] for color in range(colors)]
 
 
 def reduce_kernel(plan, terms_ref, edges_ref, out_ref, *scratch):
@@ -359,7 +377,7 @@
     )(embedding, pairs)
     node_grad, outbound = call(
         negative_kernel,
-        (shape((nodes, width), F32), shape((parts, own_neg, width + LANES), F32)),
+        (shape((nodes, width), F32), shape((2, parts // 2, own_neg, width + LANES), F32)),
         whole(5) + [pl.BlockSpec(memory_space=pltpu.SMEM), pl.BlockSpec(memory_space=pltpu.VMEM)],
     )(embedding, negatives, degree, positive_grad, loss_a, tile_count, edge_ends[0])
     total = call(
@@ -368,9 +386,12 @@
         whole(1),
         collective=1,
         scratch_shapes=[
-            pltpu.VMEM(outbound.shape, F32),
-            pltpu.SemaphoreType.DMA((parts,)),
-            pltpu.SemaphoreType.DMA((parts,)),
+            pltpu.VMEM(outbound.shape[1:], F32),
+            pltpu.VMEM(outbound.shape[1:], F32),
+            pltpu.VMEM(outbound.shape[1:], F32),
+            pltpu.SemaphoreType.DMA((2,)),
+            pltpu.SemaphoreType.DMA((parts // 2,)),
+            pltpu.SemaphoreType.DMA((parts // 2,)),
         ],
     )(outbound)
     tiles = (relations + 1, width * width // (8 * LANES), 8, LANES)
@@ -379,10 +400,11 @@
         (shape((nodes, width), BF16), shape(tiles, F32), shape((8, LANES), F32), shape((1, LANES), F32)),
         whole(5),
     )(features, means, node_grad, total, ids)
-    plan = reduce_plan(parts, tiles[0])
+    pieces = (2 * tiles[0], tiles[1] // 2, *tiles[2:])
+    plan = reduce_plan(parts, pieces[0])
     landed, sums, copies = [], [], 0
     for dims in plan:
-        length = tiles[1]
+        length = pieces[1]
         for size, _ in dims:
             length = length // size
             landed.append(pltpu.VMEM((size - 1, length, 8, LANES), F32))
@@ -390,12 +412,12 @@
             copies += 2 * (size - 1)
     reduced = call(
         functools.partial(reduce_kernel, plan),
-        shape(tiles, F32),
+        shape(pieces, F32),
         whole(2),
         collective=2,
         scratch_shapes=landed + sums + [pltpu.SemaphoreType.DMA((copies,)), pltpu.SemaphoreType.DMA((copies,))],
-    )(terms, edges)
-    weight_grad = call(finish_kernel, shape((relations + 1, width, width), F32), whole(1))(reduced)
+    )(terms.reshape(pieces), edges)
+    weight_grad = call(finish_kernel, shape((relations + 1, width, width), F32), whole(1))(reduced.reshape(tiles))
     return (weight_grad, loss[0, 0], pre_grad)
 
 

time: 128 us -> 121 us (0.945)
  Pallas kernels: 83.5 us -> 77.4 us
    pallas_call x1, Pallas kernels: 13.8 us -> 9.81 us  [on_device(): call(functools.partial(exchange_kernel, parts), shape((own_neg, width + L...]
    pallas_call x2, Pallas kernels: 57.8 us -> 55.3 us  [the longest x1 53.9 us: on_device(): call(functools.partial(reduce_kernel, plan), shape(pieces, F32), whole(2)...]
  transfers between devices with their start and end apart: 2 -> 2, of which waited for: 1 -> 1; matrix products, arithmetic and copies ran while one was open for 2% -> 2% of each run, Pallas kernels for 4% -> 5%
where the time goes in v3:
time: 121 us; the launch traced here: 120 us
  Pallas kernels  77.4 us (64%)
  starting transfers between devices  17.7 us (15%)
  local copies, waits for them, and re-layouts  15.4 us (13%)
  waiting for transfers between devices  6.88 us (6%)
  between operations  1.42 us (1%)
  matrix products  1.32 us (1%)
    pallas_call x1, Pallas kernels, on_device(): call(functools.partial(reduce_kernel, plan), shape(pieces, F32), whole(2)...  53.9 us
    unnamed x27, local copies, waits for them, and re-layouts  11.6 us
    all_to_all x1, starting transfers between devices, on_device(): lax.all_to_all(jnp.broadcast_to(my_negs[None], (parts, own_neg, width)),...  10.4 us
    pallas_call x1, Pallas kernels, on_device(): call(functools.partial(exchange_kernel, parts), shape((own_neg, width + L...  9.81 us
    all_to_all x1, starting transfers between devices, on_device(): lax.all_to_all(outgoing.reshape(parts, per_peer, width), 'dom', split_axi...  7.32 us
    all_to_all x1, waiting for transfers between devices, on_device(): lax.all_to_all(jnp.broadcast_to(my_negs[None], (parts, own_neg, width)),...  6.87 us
    pallas_call x1, Pallas kernels, on_device(): call(functools.partial(prepare_kernel, fan), (shape((relations, nodes, sl...  4.24 us
  transfers between devices with their start and end apart: 2, of which 1 were waited for; matrix products, arithmetic and copies ran while one was open for 2% of the time, Pallas kernels for 5%

profile of v3, /device:TPU:0, one launch (start us, length us, event | category | flops | bytes accessed | tf_op | source)
XLA Modules:
  0.0 120.1 jit_solution(817454285290558320)
XLA Ops:
  0.6 0.0 copy-start.3
  0.6 0.9 copy.14
  1.5 0.1 eq.10
  1.6 1.3 %convolution_convert_fusion = bf16[128,512]{1,0:T(8,128)(2,1)S(1)} fusion(bf16[512,512]{1,0:T(8,128)(2,1)} %own_ref.3, s32[128]{0:T(128)S(1)} %eq.10), kind=kOutput, calls=%fused_computation | convolution fusion | flops 67239936 | bytes 655872 | tf_op jit(solution)/shard_map/dot_general | solution.py:22
  2.9 0.7 reshape.30
  3.6 7.3 %all-to-all-start = ((bf16[32,4,512]{2,1,0:T(4,128)(2,1)}), bf16[32,4,512]{2,1,0:T(4,128)(2,1)S(1)}, u32[]{:S(2)}, u32[]{:S(2)}) async-start(bf16[32,4,512]{2,1,0:T(4,128)(2,1)} %reshape.30), calls=%async_computation | async-start | bytes 262144 | tf_op jit(solution)/shard_map/all_to_all | solution.py:350
  11.6 0.7 copy.16.ids_ref
  12.4 0.9 copy.15.nbr_ref
  13.2 0.0 copy-start.12
  13.3 0.8 copy-done.12
  14.0 4.2 %shard_map.94 = (bf16[2,512,640]{2,1,0:T(8,128)(2,1)S(1)}, f32[512,512]{1,0:T(8,128)S(1)}, f32[512,1]{1,0:T(8,128)S(1)}) custom-call(s32[512,16]{1,0:T(8,128)S(1)} %copy.15.nbr_ref, s32[16,2,256]{2,1,0:T(2,128)S(1)} %copy-done.12, s32[1]{0:T(128)S(6)} %copy.18.count_ref), custom_call_target="tpu_custom_call" | custom-call | tf_op jit(solution)/shard_map/pallas_call | solution.py:353
  18.2 0.0 copy-start.4
  18.3 1.0 copy-done.4
  19.3 0.0 copy-start.6
  19.3 1.0 copy-done.6
  20.3 0.0 copy-start.10
  20.3 0.7 copy-done.10
  21.0 0.0 all-to-all-done
  21.0 0.0 copy-done.3
  21.0 0.0 copy-start
  21.1 1.0 copy-done
  22.1 0.0 copy-start.5
  22.1 1.3 %copy-done.5 = bf16[2,512,640]{2,1,0:T(8,128)(2,1)S(1)} copy-done((bf16[2,512,640]{2,1,0:T(8,128)(2,1)S(1)}, bf16[2,512,640]{2,1,0:T(8,128)(2,1)}, u32[]{:S(2)}) %copy-start.5) | copy-done | bytes 1310744
  23.4 1.9 %shard_map.95 = (bf16[2,512,512]{2,1,0:T(8,128)(2,1)S(1)}, bf16[512,512]{1,0:T(8,128)(2,1)S(1)}, bf16[8,512]{1,0:T(8,128)(2,1)S(1)}) custom-call(bf16[512,512]{1,0:T(8,128)(2,1)S(1)} %copy-done, bf16[128,512]{1,0:T(8,128)(2,1)S(1)} %reshape.31.halo_ref, bf16[3,512,512]{2,1,0:T(8,128)(2,1)S(1)} %copy-done.3, bf16[2,512,640]{2,1,0:T(8,128)(2,1)S(1)} %copy-done.5, ...), custom_call_target="tpu_custom_call" | custom-call | tf_op jit(solution)/shard_map/pallas_call | solution.py:363
  25.3 0.0 copy-start.8
  25.3 1.0 copy-done.8
  26.3 0.0 copy-start.1
  26.3 0.7 broadcast_in_dim.2
  27.0 10.4 %all-to-all-start.1 = ((bf16[32,8,512]{2,1,0:T(8,128)(2,1)}), bf16[32,8,512]{2,1,0:T(8,128)(2,1)S(1)}, u32[]{:S(2)}, u32[]{:S(2)}) async-start(bf16[32,8,512]{2,1,0:T(8,128)(2,1)} %broadcast_in_dim.2), calls=%async_computation.1 | async-start | bytes 524288 | tf_op jit(solution)/shard_map/all_to_all | solution.py:372
  37.4 0.7 slice_bitcast_fusion.edge_ref
  38.1 0.0 copy-start.7
  38.1 1.2 %copy-done.7 = f32[512,512]{1,0:T(8,128)S(1)} copy-done((f32[512,512]{1,0:T(8,128)S(1)}, f32[512,512]{1,0:T(8,128)}, u32[]{:S(2)}) %copy-start.7) | copy-done | bytes 1048600
  39.3 0.0 copy-start.9
  39.3 1.8 %shard_map.96 = (f32[512,512]{1,0:T(8,128)S(1)}, f32[1,512]{1,0:T(1,128)S(1)}) custom-call(bf16[512,512]{1,0:T(8,128)(2,1)S(1)} %get-tuple-element.19.embed_ref, f32[512,512]{1,0:T(8,128)S(1)} %copy-done.7), custom_call_target="tpu_custom_call" | custom-call | tf_op jit(solution)/shard_map/pallas_call | solution.py:375
  41.1 6.9 %all-to-all-done.1 = bf16[32,8,512]{2,1,0:T(8,128)(2,1)S(1)} async-done(((bf16[32,8,512]{2,1,0:T(8,128)(2,1)}), bf16[32,8,512]{2,1,0:T(8,128)(2,1)S(1)}, u32[]{:S(2)}, u32[]{:S(2)}) %all-to-all-start.1) | async-done | bytes 262176 | tf_op jit(solution)/shard_map/all_to_all | solution.py:372
  48.0 0.0 copy-start.11
  48.0 0.9 copy-done.11
  48.9 1.4 %shard_map.97 = (f32[512,512]{1,0:T(8,128)S(1)}, f32[2,16,8,640]{3,2,1,0:T(8,128)S(1)}) custom-call(bf16[512,512]{1,0:T(8,128)(2,1)S(1)} %get-tuple-element.19.embed_ref, bf16[256,512]{1,0:T(8,128)(2,1)S(1)} %bitcast.12, f32[512,1]{1,0:T(8,128)S(1)} %copy-done.11, f32[512,512]{1,0:T(8,128)S(1)} %get-tuple-element.23.positive_ref, ...), custom_call_target="tpu_custom_call" | custom-call | tf_op jit(solution)/shard_map/pallas_call | solution.py:378
  50.3 9.8 %shard_map.98.total_ref = f32[8,640]{1,0:T(8,128)S(1)} custom-call(f32[2,16,8,640]{3,2,1,0:T(8,128)S(1)} %get-tuple-element.26.send_ref), custom_call_target="tpu_custom_call" | custom-call | tf_op jit(solution)/shard_map/pallas_call | solution.py:383
  60.1 0.0 copy-done.1
  60.1 0.0 copy-done.9
  60.1 2.3 %shard_map.99 = (bf16[512,512]{1,0:T(8,128)(2,1)}, f32[3,256,8,128]{3,2,1,0:T(8,128)S(1)}, f32[8,128]{1,0:T(8,128)S(1)}, f32[1,128]{1,0:T(1,128)}) custom-call(bf16[512,512]{1,0:T(8,128)(2,1)S(1)} %copy-done.1, bf16[2,512,512]{2,1,0:T(8,128)(2,1)S(1)} %copy-done.9, f32[512,512]{1,0:T(8,128)S(1)} %get-tuple-element.25.grad_ref, ...), custom_call_target="tpu_custom_call" | custom-call | tf_op jit(solution)/shard_map/pallas_call | solution.py:398
  62.5 0.0 copy-start.2
  62.5 1.7 %copy-done.2 = f32[3,256,8,128]{3,2,1,0:T(8,128)} copy-done((f32[3,256,8,128]{3,2,1,0:T(8,128)}, f32[3,256,8,128]{3,2,1,0:T(8,128)S(1)}, u32[]{:S(2)}) %copy-start.2) | copy-done | bytes 3145752
  64.1 53.9 %shard_map.100 = f32[6,128,8,128]{3,2,1,0:T(8,128)S(1)} custom-call(f32[6,128,8,128]{3,2,1,0:T(8,128)} %bitcast.11, f32[8,128]{1,0:T(8,128)S(1)} %get-tuple-element.28.edges_ref), custom_call_target="tpu_custom_call" | custom-call | tf_op jit(solution)/shard_map/pallas_call | solution.py:413
  118.0 2.1 %shard_map.101 = f32[3,512,512]{2,1,0:T(8,128)} custom-call(f32[3,256,8,128]{3,2,1,0:T(8,128)S(1)} %bitcast.10), custom_call_target="tpu_custom_call" | custom-call | tf_op jit(solution)/shard_map/pallas_call | solution.py:420
  (1 shorter events, 0.0 us)
Async XLA Ops:
  0.6 20.4 %copy-start.3 = (bf16[3,512,512]{2,1,0:T(8,128)(2,1)S(1)}, bf16[3,512,512]{2,1,0:T(8,128)(2,1)}, u32[]{:S(2)}) copy-start(bf16[3,512,512]{2,1,0:T(8,128)(2,1)} %weights_ref.1) | copy-start | bytes 4718596
  3.6 17.4 %all-to-all-start = ((bf16[32,4,512]{2,1,0:T(4,128)(2,1)}), bf16[32,4,512]{2,1,0:T(4,128)(2,1)S(1)}, u32[]{:S(2)}, u32[]{:S(2)}) async-start(bf16[32,4,512]{2,1,0:T(4,128)(2,1)} %reshape.30), calls=%async_computation | async-start | bytes 262144 | tf_op jit(solution)/shard_map/all_to_all | solution.py:350
  13.2 0.8 copy-start.12
  18.2 1.1 copy-start.4
  19.3 1.0 copy-start.6
  20.3 0.7 copy-start.10
  21.0 1.0 copy-start
  22.1 1.3 %copy-start.5 = (bf16[2,512,640]{2,1,0:T(8,128)(2,1)S(1)}, bf16[2,512,640]{2,1,0:T(8,128)(2,1)}, u32[]{:S(2)}) copy-start(bf16[2,512,640]{2,1,0:T(8,128)(2,1)} %copy-done.4) | copy-start | bytes 3932164
  25.3 1.0 copy-start.8
  26.3 33.9 %copy-start.1 = (bf16[512,512]{1,0:T(8,128)(2,1)S(1)}, bf16[512,512]{1,0:T(8,128)(2,1)}, u32[]{:S(2)}) copy-start(bf16[512,512]{1,0:T(8,128)(2,1)} %own_ref.3) | copy-start | bytes 1572868
  27.0 21.0 %all-to-all-start.1 = ((bf16[32,8,512]{2,1,0:T(8,128)(2,1)}), bf16[32,8,512]{2,1,0:T(8,128)(2,1)S(1)}, u32[]{:S(2)}, u32[]{:S(2)}) async-start(bf16[32,8,512]{2,1,0:T(8,128)(2,1)} %broadcast_in_dim.2), calls=%async_computation.1 | async-start | bytes 524288 | tf_op jit(solution)/shard_map/all_to_all | solution.py:372
  38.1 1.2 %copy-start.7 = (f32[512,512]{1,0:T(8,128)S(1)}, f32[512,512]{1,0:T(8,128)}, u32[]{:S(2)}) copy-start(f32[512,512]{1,0:T(8,128)} %copy-done.6) | copy-start | bytes 3145732
  39.3 20.8 %copy-start.9 = (bf16[2,512,512]{2,1,0:T(8,128)(2,1)S(1)}, bf16[2,512,512]{2,1,0:T(8,128)(2,1)}, u32[]{:S(2)}) copy-start(bf16[2,512,512]{2,1,0:T(8,128)(2,1)} %copy-done.8) | copy-start | bytes 3145732
  48.0 1.0 copy-start.11
  62.5 1.7 %copy-start.2 = (f32[3,256,8,128]{3,2,1,0:T(8,128)}, f32[3,256,8,128]{3,2,1,0:T(8,128)S(1)}, u32[]{:S(2)}) copy-start(f32[3,256,8,128]{3,2,1,0:T(8,128)S(1)} %get-tuple-element.27) | copy-start | bytes 9437188
